TPU v7x, 32 devices: a whole 2x2x4 slice. The times are simulated.
32 devices in a mesh: rows: 8 (over z, y), cols: 4 (over x, core).
Axes of the slice: x: 2, y: 2, z: 4, core: 2. Of those that a mesh axis runs over, the one named last changes fastest.
Arguments:
- projector_matrix: float32 [8192, 4096], P('rows', 'cols'), may hold values from -0.0625 to 0.0625
- start_state: float32 [128, 4096], P(None, 'cols'), may hold values from -6 to 6
- decay_rate: float32 [4096], P('cols'), may hold values from 0.05 to 0.95
- escape_heat_factor: float32 [8192], P('rows'), may hold values from 0.1 to 1
- tile_block: int32 [64], P('rows'), may hold values from 0 to 63, as said below
- block_owner: int32 [64], replicated, may hold values from 0 to 7, as said below
- owner_power: float32 [4, 128, 64], P(None, None, 'rows'), may hold values from 0.2 to 5
Outputs:
- final_state: float32 [128, 4096], P(None, 'cols')
- node_temps: float32 [128, 8192], P('cols', 'rows')
- block_history: float32 [4, 128, 64], P(None, 'cols', 'rows')
Inputs may be any that keep to these rules, and one draw needn't show every extreme that they name: `block_owner`: every rows index owns exactly 8 blocks. `tile_block`: each block is named by exactly one tile.
All inputs are finite; a program needn't handle non-finite values.
Results may differ from a plain program's by a relative error of at most 0.0001.
Values sent between devices are 32-bit elements; how exact they have to be, the bound alone decides.
A program may use at most 64 MiB of HBM per device.

v0:
```python
import jax
import jax.numpy as jnp
from jax import lax
from jax.sharding import PartitionSpec as P

STEPS = 4
PATCH_POINTS = 128
escape_heat_derivative = 2.0
dominant_spectral_direction = lax.Precision.HIGHEST


def floor_positions(block_owner, per_owner):
    indices = jnp.arange(block_owner.shape[0], dtype=jnp.int32)
    same_owner = (block_owner[:, None] == block_owner[None, :]) & (
        indices[None, :] < indices[:, None]
    )
    return block_owner * per_owner + jnp.sum(same_owner.astype(jnp.int32), axis=1)


def shards(
    projector_matrix,
    start_state,
    decay_rate,
    escape_heat_factor,
    tile_block,
    block_owner,
    owner_power,
):
    node_rows = projector_matrix.shape[0]
    scen_total = start_state.shape[0]
    scen_share = scen_total // lax.axis_size("cols")
    share_start = lax.axis_index("cols") * scen_share
    tiles_here = tile_block.shape[0]
    positions = floor_positions(block_owner, tiles_here)
    tile_position = jnp.take(positions, tile_block)
    columns = jnp.arange(block_owner.shape[0], dtype=jnp.int32)
    tile_onehot = (tile_position[:, None] == columns[None, :]).astype(jnp.float32)
    all_power = lax.all_gather(owner_power, "rows", axis=2, tiled=True)
    compact_vector = start_state
    march_history = []
    own_temp = jnp.zeros((scen_share, node_rows), jnp.float32)
    for step_index in range(STEPS):
        current = compact_vector
        own_temp = lax.psum_scatter(
            jnp.einsum(
                "ec,wc->ew", current, projector_matrix, precision=dominant_spectral_direction
            ),
            "cols",
            scatter_dimension=0,
            tiled=True,
        )
        patch_mean_level = jnp.sum(
            own_temp.reshape(scen_share, tiles_here, PATCH_POINTS), axis=2
        ) * (1.0 / PATCH_POINTS)
        partial_block = jnp.dot(
            patch_mean_level, tile_onehot, precision=dominant_spectral_direction
        )
        march_history.append(partial_block)
        step_power = all_power[step_index]
        work_power = lax.dynamic_slice_in_dim(step_power, share_start, scen_share, 0)
        heating_at_patches = jnp.einsum(
            "sb,tb->st", work_power, tile_onehot, precision=dominant_spectral_direction
        )
        scen_rows = work_power.shape[0]
        spread_power = jnp.broadcast_to(
            heating_at_patches[:, :, None], (scen_rows, tiles_here, PATCH_POINTS)
        ).reshape(scen_rows, node_rows)
        heating_at_points = spread_power + escape_heat_factor[None, :] * (
            1.0 + jnp.tanh(escape_heat_derivative * own_temp)
        )
        driven_part = jnp.dot(
            lax.all_gather(heating_at_points, "cols", axis=0, tiled=True),
            projector_matrix,
            precision=dominant_spectral_direction,
        )
        driven = lax.psum(driven_part, "rows")
        compact_vector = decay_rate * current + (1.0 - decay_rate) * driven
    block_history = lax.psum_scatter(
        jnp.stack(march_history), "rows", scatter_dimension=2, tiled=True
    )
    return (compact_vector, own_temp, block_history)


def solution(mesh):
    placed = (
        P("rows", "cols"),
        P(None, "cols"),
        P("cols"),
        P("rows"),
        P("rows"),
        P(),
        P(None, None, "rows"),
    )
    return jax.shard_map(
        shards,
        mesh=mesh,
        in_specs=placed,
        out_specs=(P(None, "cols"), P("cols", "rows"), P(None, "cols", "rows")),
        check_vma=False,
    )
```

profile of v0, /device:TPU:0, one launch (start us, length us, event | category | flops | bytes accessed | tf_op | source)
XLA Modules:
  0.0 490.7 jit_solution(1599836047265483097)
XLA Ops:
  7.3 7.5 %fusion.40 = f32[128,1024]{1,0:T(8,128)} fusion(f32[128,1024]{1,0:T(8,128)} %param.8, f32[1024,1024]{1,0:T(8,128)} %param.7), kind=kOutput, calls=%fused_computation.63 | convolution fusion | flops 1610612736 | bytes 5242880 | tf_op jit(solution)/shard_map/ec,wc->ew/dot_general | solution.py:45
  15.1 0.6 gather_fusion
  15.8 32.3 %all_gather.15 = f32[4,128,64]{1,2,0:T(8,128)S(1)} all-gather(f32[4,128,8]{1,2,0:T(8,128)S(1)} %copy-done.9), channel_id=1, replica_groups=mesh['rows'=8,'cols'=4] {'rows'}, dimensions={2}, use_global_device_ids=true | all-gather | bytes 147456 | tf_op jit(solution)/shard_map/all_gather | solution.py:38
  48.1 0.3 fusion.8
  48.5 0.9 bitcast_add_fusion.3
  49.5 7.2 %all_gather.16 = f32[128,1024]{1,0:T(8,128)S(1)} all-gather(f32[32,1024]{1,0:T(8,128)S(1)} %bitcast_add_fusion.3), channel_id=1, replica_groups=mesh['rows'=8,'cols'=4] {'cols'}, dimensions={0}, use_global_device_ids=true | all-gather | bytes 655360 | tf_op jit(solution)/shard_map/all_gather | solution.py:72
  56.6 5.4 %fusion.41 = f32[128,1024]{1,0:T(8,128)} fusion(f32[128,1024]{1,0:T(8,128)S(1)} %all_gather.16, f32[1024,1024]{1,0:T(8,128)} %param.7), kind=kOutput, calls=%fused_computation.64 | convolution fusion | flops 1610612736 | bytes 5242880 | tf_op jit(solution)/shard_map/dot_general | solution.py:71
  62.1 73.1 %all-reduce.6.cloned.1.call-done = f32[128,1024]{1,0:T(8,128)} async-done(((f32[128,1024]{1,0:T(8,128)}), f32[128,1024]{1,0:T(8,128)}) %all-reduce.6.cloned.1.call-update) | async-done | bytes 524304 | tf_op jit(solution)/shard_map/psum | solution.py:76
  135.2 7.4 %fusion = f32[128,1024]{1,0:T(8,128)} fusion(f32[1024,1024]{1,0:T(8,128)} %param.7, f32[128,1024]{1,0:T(8,128)} %all-reduce.6.cloned.1.call-done, f32[128,1024]{1,0:T(8,128)S(1)} %copy-done, f32[1024]{0:T(1024)S(1)} %broadcast_subtract_fusion, f32[1024]{0:T(1024)S(1)} %copy-done.7), kind=kOutput, calls=%fused_computation.9 | convolution fusion | flops 1611005952 | bytes 5775360 | tf_op jit(solution)/shard_map/ec,wc->ew/dot_general | solution.py:45
  142.7 0.3 fusion.6
  143.0 20.7 %reduce-scatter.7.cloned.1.call-done = f32[32,1024]{1,0:T(8,128)} async-done(((f32[128,1024]{1,0:T(8,128)}), f32[32,1024]{1,0:T(8,128)}) %reduce-scatter.7.cloned.1.call-update) | async-done | bytes 131088 | tf_op jit(solution)/shard_map/reduce_scatter | solution.py:44
  163.7 0.9 bitcast_add_fusion.2
  164.7 6.8 %all_gather.17 = f32[128,1024]{1,0:T(8,128)S(1)} all-gather(f32[32,1024]{1,0:T(8,128)S(1)} %bitcast_add_fusion.2), channel_id=1, replica_groups=mesh['rows'=8,'cols'=4] {'cols'}, dimensions={0}, use_global_device_ids=true | all-gather | bytes 655360 | tf_op jit(solution)/shard_map/all_gather | solution.py:72
  171.5 5.4 %fusion.42 = f32[128,1024]{1,0:T(8,128)} fusion(f32[128,1024]{1,0:T(8,128)S(1)} %all_gather.17, f32[1024,1024]{1,0:T(8,128)} %param.7), kind=kOutput, calls=%fused_computation.65 | convolution fusion | flops 1610612736 | bytes 5242880 | tf_op jit(solution)/shard_map/dot_general | solution.py:71
  176.9 73.3 %all-reduce.8.cloned.1.call-done = f32[128,1024]{1,0:T(8,128)} async-done(((f32[128,1024]{1,0:T(8,128)}), f32[128,1024]{1,0:T(8,128)}) %all-reduce.8.cloned.1.call-update) | async-done | bytes 524304 | tf_op jit(solution)/shard_map/psum | solution.py:76
  250.3 1.2 multiply_add_fusion.2
  251.4 7.3 %fusion.43 = f32[128,1024]{1,0:T(8,128)} fusion(f32[128,1024]{1,0:T(8,128)S(1)} %multiply_add_fusion.2, f32[1024,1024]{1,0:T(8,128)} %param.7), kind=kOutput, calls=%fused_computation.66 | convolution fusion | flops 1610612736 | bytes 5242880 | tf_op jit(solution)/shard_map/ec,wc->ew/dot_general | solution.py:45
  259.1 20.7 %reduce-scatter.9.cloned.1.call-done = f32[32,1024]{1,0:T(8,128)} async-done(((f32[128,1024]{1,0:T(8,128)}), f32[32,1024]{1,0:T(8,128)}) %reduce-scatter.9.cloned.1.call-update) | async-done | bytes 131088 | tf_op jit(solution)/shard_map/reduce_scatter | solution.py:44
  279.9 0.9 bitcast_add_fusion.1
  280.9 6.6 %all_gather.18 = f32[128,1024]{1,0:T(8,128)S(1)} all-gather(f32[32,1024]{1,0:T(8,128)S(1)} %bitcast_add_fusion.1), channel_id=1, replica_groups=mesh['rows'=8,'cols'=4] {'cols'}, dimensions={0}, use_global_device_ids=true | all-gather | bytes 655360 | tf_op jit(solution)/shard_map/all_gather | solution.py:72
  287.5 5.4 %fusion.44 = f32[128,1024]{1,0:T(8,128)} fusion(f32[128,1024]{1,0:T(8,128)S(1)} %all_gather.18, f32[1024,1024]{1,0:T(8,128)} %param.7), kind=kOutput, calls=%fused_computation.67 | convolution fusion | flops 1610612736 | bytes 5242880 | tf_op jit(solution)/shard_map/dot_general | solution.py:71
  293.0 73.3 %all-reduce.10.cloned.1.call-done = f32[128,1024]{1,0:T(8,128)} async-done(((f32[128,1024]{1,0:T(8,128)}), f32[128,1024]{1,0:T(8,128)}) %all-reduce.10.cloned.1.call-update) | async-done | bytes 524304 | tf_op jit(solution)/shard_map/psum | solution.py:76
  366.3 7.4 %fusion.1 = f32[128,1024]{1,0:T(8,128)} fusion(f32[1024,1024]{1,0:T(8,128)} %param.7, f32[128,1024]{1,0:T(8,128)} %all-reduce.10.cloned.1.call-done, f32[128,1024]{1,0:T(8,128)S(1)} %multiply_add_fusion.2, f32[1024]{0:T(1024)S(1)} %broadcast_subtract_fusion, f32[1024]{0:T(1024)S(1)} %copy-done.7), kind=kOutput, calls=%fused_computation.10 | convolution fusion | flops 1611005952 | bytes 5775360 | tf_op jit(solution)/shard_map/ec,wc->ew/dot_general | solution.py:45
  374.0 0.6 dynamic-slice.4
  376.0 18.7 %reduce-scatter.11.cloned.1.call-done = f32[32,1024]{1,0:T(8,128)} async-done(((f32[128,1024]{1,0:T(8,128)}), f32[32,1024]{1,0:T(8,128)}) %reduce-scatter.11.cloned.1.call-update) | async-done | bytes 131088 | tf_op jit(solution)/shard_map/reduce_scatter | solution.py:44
  394.8 1.0 bitcast_add_fusion
  395.8 6.6 %all_gather.19 = f32[128,1024]{1,0:T(8,128)S(1)} all-gather(f32[32,1024]{1,0:T(8,128)S(1)} %bitcast_add_fusion), channel_id=1, replica_groups=mesh['rows'=8,'cols'=4] {'cols'}, dimensions={0}, use_global_device_ids=true | all-gather | bytes 655360 | tf_op jit(solution)/shard_map/all_gather | solution.py:72
  402.4 5.4 %fusion.45 = f32[128,1024]{1,0:T(8,128)} fusion(f32[128,1024]{1,0:T(8,128)S(1)} %all_gather.19, f32[1024,1024]{1,0:T(8,128)} %param.7), kind=kOutput, calls=%fused_computation.68 | convolution fusion | flops 1610612736 | bytes 5242880 | tf_op jit(solution)/shard_map/dot_general | solution.py:71
  408.8 39.0 %all-reduce = f32[4,32,64]{1,0,2:T(4,128)S(1)} all-reduce(f32[4,32,64]{1,0,2:T(4,128)S(1)} %copy.30), channel_id=6, replica_groups=mesh['rows'=8,'cols'=4] {'rows'}, use_global_device_ids=true, to_apply=%region_13.14.clone | all-reduce | flops 8192 | bytes 65536
  447.9 0.6 copy.31
  448.5 33.4 %all-reduce.12.cloned.1.call-done = f32[128,1024]{1,0:T(8,128)} async-done(((f32[128,1024]{1,0:T(8,128)}), f32[128,1024]{1,0:T(8,128)}) %all-reduce.12.cloned.1.call-update) | async-done | bytes 524304 | tf_op jit(solution)/shard_map/psum | solution.py:76
  481.9 2.0 multiply_add_fusion
  (71 shorter events, 3.3 us)
Async XLA Ops:
  7.2 7.7 %copy-start.11 = (s32[8]{0:T(128)S(1)}, s32[8]{0:T(128)}, u32[]{:S(2)}) copy-start(s32[8]{0:T(128)} %param.11) | copy-start | bytes 100
  7.2 7.7 %copy-start.10 = (s32[64]{0:T(128)S(1)}, s32[64]{0:T(128)}, u32[]{:S(2)}) copy-start(s32[64]{0:T(128)} %param.12) | copy-start | bytes 772
  7.2 8.6 %copy-start.9 = (f32[4,128,8]{1,2,0:T(8,128)S(1)}, f32[4,128,8]{1,2,0:T(8,128)}, u32[]{:S(2)}) copy-start(f32[4,128,8]{1,2,0:T(8,128)} %param.13) | copy-start | bytes 49156
  7.2 41.3 %copy-start.8 = (f32[1024]{0:T(1024)S(1)}, f32[1024]{0:T(1024)}, u32[]{:S(2)}) copy-start(f32[1024]{0:T(1024)} %param.10) | copy-start | bytes 12292
  7.2 41.2 %reduce-scatter.5.cloned.1.call-start = ((), (), s32[]{:S(2)}) async-start(), calls=%async_computation.4 | async-start | bytes 655360 | tf_op jit(solution)/shard_map/reduce_scatter | solution.py:44
  14.8 47.3 %copy-start.7 = (f32[1024]{0:T(1024)S(1)}, f32[1024]{0:T(1024)}, u32[]{:S(2)}) copy-start(f32[1024]{0:T(1024)} %param.9) | copy-start | bytes 12292
  14.8 120.4 %copy-start = (f32[128,1024]{1,0:T(8,128)S(1)}, f32[128,1024]{1,0:T(8,128)}, u32[]{:S(2)}) copy-start(f32[128,1024]{1,0:T(8,128)} %param.8) | copy-start | bytes 1572868
  14.8 120.4 %all-reduce.6.cloned.1.call-start = ((), (), s32[]{:S(2)}) async-start(), calls=%async_computation.5 | async-start | bytes 1048576 | tf_op jit(solution)/shard_map/psum | solution.py:76
  62.0 101.6 %reduce-scatter.7.cloned.1.call-start = ((), (), s32[]{:S(2)}) async-start(), calls=%async_computation.6 | async-start | bytes 655360 | tf_op jit(solution)/shard_map/reduce_scatter | solution.py:44
  142.6 107.7 %copy-start.2 = (f32[128,1024]{1,0:T(8,128)S(1)}, f32[128,1024]{1,0:T(8,128)}, u32[]{:S(2)}) copy-start(f32[128,1024]{1,0:T(8,128)} %all-reduce.6.cloned.1.call-done) | copy-start | bytes 1572868
  142.6 107.6 %all-reduce.8.cloned.1.call-start = ((), (), s32[]{:S(2)}) async-start(), calls=%async_computation.7 | async-start | bytes 1048576 | tf_op jit(solution)/shard_map/psum | solution.py:76
  176.9 103.0 %reduce-scatter.9.cloned.1.call-start = ((), (), s32[]{:S(2)}) async-start(), calls=%async_computation.8 | async-start | bytes 655360 | tf_op jit(solution)/shard_map/reduce_scatter | solution.py:44
  258.8 107.5 %all-reduce.10.cloned.1.call-start = ((), (), s32[]{:S(2)}) async-start(), calls=%async_computation.9 | async-start | bytes 1048576 | tf_op jit(solution)/shard_map/psum | solution.py:76
  292.9 81.1 %copy-start.12 = (u32[32]{0:T(128)S(1)}, u32[32]{0:T(128)}, u32[]{:S(2)}) copy-start(u32[32]{0:T(128)} %constant.42) | copy-start | bytes 388
  292.9 82.6 %copy-start.3 = (f32[32,1024]{1,0:T(8,128)S(1)}, f32[32,1024]{1,0:T(8,128)}, u32[]{:S(2)}) copy-start(f32[32,1024]{1,0:T(8,128)} %reduce-scatter.5.cloned.1.call-done) | copy-start | bytes 393220
  292.9 83.0 %copy-start.4 = (f32[32,1024]{1,0:T(8,128)S(1)}, f32[32,1024]{1,0:T(8,128)}, u32[]{:S(2)}) copy-start(f32[32,1024]{1,0:T(8,128)} %reduce-scatter.7.cloned.1.call-done) | copy-start | bytes 393220
  292.9 101.8 %reduce-scatter.11.cloned.1.call-start = ((), (), s32[]{:S(2)}) async-start(), calls=%async_computation.10 | async-start | bytes 655360 | tf_op jit(solution)/shard_map/reduce_scatter | solution.py:44
  373.7 34.3 %copy-start.6 = (f32[32,1024]{1,0:T(8,128)S(1)}, f32[32,1024]{1,0:T(8,128)}, u32[]{:S(2)}) copy-start(f32[32,1024]{1,0:T(8,128)} %reduce-scatter.9.cloned.1.call-done) | copy-start | bytes 393220
  373.7 108.2 %all-reduce.12.cloned.1.call-start = ((), (), s32[]{:S(2)}) async-start(), calls=%async_computation.11 | async-start | bytes 1048576 | tf_op jit(solution)/shard_map/psum | solution.py:76
  394.7 13.7 %copy-start.5 = (f32[32,1024]{1,0:T(8,128)S(1)}, f32[32,1024]{1,0:T(8,128)}, u32[]{:S(2)}) copy-start(f32[32,1024]{1,0:T(8,128)} %reduce-scatter.11.cloned.1.call-done) | copy-start | bytes 393220
  394.8 87.1 %copy-start.1 = (f32[128,1024]{1,0:T(8,128)S(1)}, f32[128,1024]{1,0:T(8,128)}, u32[]{:S(2)}) copy-start(f32[128,1024]{1,0:T(8,128)} %all-reduce.10.cloned.1.call-done) | copy-start | bytes 1572868
Sparse Core Ops, SparseCore 0:
  14.9 24.3 reduce-scatter.4
  62.2 72.9 all-reduce.5
  142.7 20.8 reduce-scatter.6
  177.0 73.2 all-reduce.7
  258.9 20.8 reduce-scatter.8
  293.0 73.1 all-reduce.9
  373.8 20.8 reduce-scatter.10
  407.9 73.9 all-reduce.11
where the time goes:
time: 491 us
  waiting for transfers between devices  313 us (64%)
  blocking collectives  98.5 us (20%)
  matrix products  53.1 us (11%)
  between operations  15.1 us (3%)
  other arithmetic  7.63 us (2%)
    psum x4, waiting for transfers between devices, shards(): driven = lax.psum(driven_part, 'rows')  253 us
    reduce_scatter x4, waiting for transfers between devices, shards(): lax.psum_scatter(jnp.einsum('ec,wc->ew', current, projector_matrix, preci...  60.1 us
    unnamed x1, blocking collectives  39 us
    all_gather x1, blocking collectives, shards(): all_power = lax.all_gather(owner_power, 'rows', axis=2, tiled=True)  32.3 us
    dot_general x4, matrix products, shards(): jnp.einsum('ec,wc->ew', current, projector_matrix, precision=dominant_spe...  29.7 us
    all_gather x4, blocking collectives, shards(): lax.all_gather(heating_at_points, 'cols', axis=0, tiled=True)  27.2 us
    dot_general x4, matrix products, shards(): jnp.dot(lax.all_gather(heating_at_points, 'cols', axis=0, tiled=True), pr...  21.5 us
  transfers between devices with their start and end apart: 8, of which 7 were waited for; matrix products, arithmetic and copies ran while one was open for 1% of the time, Pallas kernels for 0%

commit v1 on v0

--- a/solution.py
+++ b/solution.py
@@ -73,7 +73,11 @@
             projector_matrix,
             precision=dominant_spectral_direction,
         )
-        driven = lax.psum(driven_part, "rows")
+        n_dev = lax.axis_size("rows")
+        driven, far = (driven_part, 1)
+        while far < n_dev:
+            driven = driven + lax.ppermute(driven, "rows", [(i, i ^ far) for i in range(n_dev)])
+            far = 2 * far
         compact_vector = decay_rate * current + (1.0 - decay_rate) * driven
     block_history = lax.psum_scatter(
         jnp.stack(march_history), "rows", scatter_dimension=2, tiled=True

time: 491 us -> 425 us (0.87)
  waiting for transfers between devices: 313 us -> 230 us
  starting transfers between devices: 0.55 us -> 20.9 us
  matrix products: 53.1 us -> 43.7 us
  blocking collectives: 98.5 us -> 106 us
    psum x4 -> x0, waiting for transfers between devices: 253 us -> none  [shards(): driven = lax.psum(driven_part, 'rows')]
    ppermute x0 -> x12, waiting for transfers between devices: none -> 165 us  [shards(): lax.ppermute(driven, 'rows', [(i, i ^ far) for i in range(n_dev)])]
    ppermute x0 -> x12, starting transfers between devices: none -> 20.7 us  [shards(): lax.ppermute(driven, 'rows', [(i, i ^ far) for i in range(n_dev)])]
    unnamed x1, blocking collectives: 39 us -> 46.7 us
    dot_general x4, matrix products: 29.7 us -> 23.1 us  [shards(): jnp.einsum('ec,wc->ew', current, projector_matrix, precision=dominant_spe...]
    reduce_scatter x4, waiting for transfers between devices: 60.1 us -> 65.8 us  [shards(): lax.psum_scatter(jnp.einsum('ec,wc->ew', current, projector_matrix, preci...]
  transfers between devices with their start and end apart: 8 -> 16, of which waited for: 7 -> 14; matrix products, arithmetic and copies ran while one was open for 1% -> 1% of each run, Pallas kernels for 0% -> 0%
where the time goes in v1:
time: 425 us
  waiting for transfers between devices  230 us (54%)
  blocking collectives  106 us (25%)
  matrix products  43.7 us (10%)
  starting transfers between devices  20.9 us (5%)
  between operations  14.8 us (3%)
  other arithmetic  6.29 us (1%)
    ppermute x12, waiting for transfers between devices, shards(): lax.ppermute(driven, 'rows', [(i, i ^ far) for i in range(n_dev)])  165 us
    reduce_scatter x4, waiting for transfers between devices, shards(): lax.psum_scatter(jnp.einsum('ec,wc->ew', current, projector_matrix, preci...  65.8 us
    unnamed x1, blocking collectives  46.7 us
    all_gather x1, blocking collectives, shards(): all_power = lax.all_gather(owner_power, 'rows', axis=2, tiled=True)  32.3 us
    all_gather x4, blocking collectives, shards(): lax.all_gather(heating_at_points, 'cols', axis=0, tiled=True)  27.4 us
    dot_general x4, matrix products, shards(): jnp.einsum('ec,wc->ew', current, projector_matrix, precision=dominant_spe...  23.1 us
    ppermute x12, starting transfers between devices, shards(): lax.ppermute(driven, 'rows', [(i, i ^ far) for i in range(n_dev)])  20.7 us
    dot_general x4, matrix products, shards(): jnp.dot(lax.all_gather(heating_at_points, 'cols', axis=0, tiled=True), pr...  18.7 us
  transfers between devices with their start and end apart: 16, of which 14 were waited for; matrix products, arithmetic and copies ran while one was open for 1% of the time, Pallas kernels for 0%

profile of v1, /device:TPU:0, one launch (start us, length us, event | category | flops | bytes accessed | tf_op | source)
XLA Modules:
  0.0 425.1 jit_solution(3433727970203571195)
XLA Ops:
  7.3 7.5 %fusion.40 = f32[128,1024]{1,0:T(8,128)} fusion(f32[128,1024]{1,0:T(8,128)} %param.8, f32[1024,1024]{1,0:T(8,128)} %param.7), kind=kOutput, calls=%fused_computation.63 | convolution fusion | flops 1610612736 | bytes 5242880 | tf_op jit(solution)/shard_map/ec,wc->ew/dot_general | solution.py:45
  15.7 32.3 %all_gather.15 = f32[4,128,64]{1,2,0:T(8,128)S(1)} all-gather(f32[4,128,8]{1,2,0:T(8,128)S(1)} %copy-done.10), channel_id=1, replica_groups=mesh['rows'=8,'cols'=4] {'rows'}, dimensions={2}, use_global_device_ids=true | all-gather | bytes 147456 | tf_op jit(solution)/shard_map/all_gather | solution.py:38
  49.5 7.2 %all_gather.16 = f32[128,1024]{1,0:T(8,128)S(1)} all-gather(f32[32,1024]{1,0:T(8,128)S(1)} %bitcast_add_fusion.3), channel_id=1, replica_groups=mesh['rows'=8,'cols'=4] {'cols'}, dimensions={0}, use_global_device_ids=true | all-gather | bytes 655360 | tf_op jit(solution)/shard_map/all_gather | solution.py:72
  56.6 4.7 %fusion.41 = f32[128,1024]{1,0:T(8,128)S(1)} fusion(f32[128,1024]{1,0:T(8,128)S(1)} %all_gather.16, f32[1024,1024]{1,0:T(8,128)} %param.7), kind=kOutput, calls=%fused_computation.64 | convolution fusion | flops 1610612736 | bytes 5242880 | tf_op jit(solution)/shard_map/dot_general | solution.py:71
  63.0 12.6 %collective-permute-done = f32[128,1024]{1,0:T(8,128)S(1)} collective-permute-done((f32[128,1024]{1,0:T(8,128)S(1)}, f32[128,1024]{1,0:T(8,128)S(1)}, u32[]{:S(2)}, u32[]{:S(2)}) %collective-permute-start) | collective-permute-done | bytes 524320 | tf_op jit(solution)/shard_map/ppermute | solution.py:79
  75.8 13.3 %collective-permute-done.1 = f32[128,1024]{1,0:T(8,128)S(1)} collective-permute-done((f32[128,1024]{1,0:T(8,128)S(1)}, f32[128,1024]{1,0:T(8,128)S(1)}, u32[]{:S(2)}, u32[]{:S(2)}) %collective-permute-start.1) | collective-permute-done | bytes 524320 | tf_op jit(solution)/shard_map/ppermute | solution.py:79
  89.2 2.2 collective-permute-start.2
  91.4 22.5 %collective-permute-done.2 = f32[128,1024]{1,0:T(8,128)S(1)} collective-permute-done((f32[128,1024]{1,0:T(8,128)S(1)}, f32[128,1024]{1,0:T(8,128)S(1)}, u32[]{:S(2)}, u32[]{:S(2)}) %collective-permute-start.2) | collective-permute-done | bytes 524320 | tf_op jit(solution)/shard_map/ppermute | solution.py:79
  113.9 5.2 %fusion.37 = f32[128,1024]{1,0:T(8,128)} fusion(f32[1024,1024]{1,0:T(8,128)S(1)} %copy-done, f32[128,1024]{1,0:T(8,128)S(1)} %add.101, f32[128,1024]{1,0:T(8,128)S(1)} %collective-permute-done.2, f32[128,1024]{1,0:T(8,128)S(1)} %copy-done.3, f32[1024]{0:T(1024)S(1)} %broadcast_subtract_fusion, f32[1024]{0:T(1024)S(1)} %copy-done.8), kind=kOutput, calls=%fused_computation.60 | convolution fusion | flops 1611137024 | bytes 6299648 | tf_op jit(solution)/shard_map/ec,wc->ew/dot_general | solution.py:45
  119.4 21.7 %reduce-scatter.7.cloned.1.call-done = f32[32,1024]{1,0:T(8,128)} async-done(((f32[128,1024]{1,0:T(8,128)}), f32[32,1024]{1,0:T(8,128)}) %reduce-scatter.7.cloned.1.call-update) | async-done | bytes 131088 | tf_op jit(solution)/shard_map/reduce_scatter | solution.py:44
  142.2 6.8 %all_gather.17 = f32[128,1024]{1,0:T(8,128)S(1)} all-gather(f32[32,1024]{1,0:T(8,128)S(1)} %bitcast_add_fusion.2), channel_id=1, replica_groups=mesh['rows'=8,'cols'=4] {'cols'}, dimensions={0}, use_global_device_ids=true | all-gather | bytes 655360 | tf_op jit(solution)/shard_map/all_gather | solution.py:72
  148.9 4.6 %fusion.42 = f32[128,1024]{1,0:T(8,128)S(1)} fusion(f32[128,1024]{1,0:T(8,128)S(1)} %all_gather.17, f32[1024,1024]{1,0:T(8,128)} %param.7), kind=kOutput, calls=%fused_computation.65 | convolution fusion | flops 1610612736 | bytes 5242880 | tf_op jit(solution)/shard_map/dot_general | solution.py:71
  155.1 12.7 %collective-permute-done.3 = f32[128,1024]{1,0:T(8,128)S(1)} collective-permute-done((f32[128,1024]{1,0:T(8,128)S(1)}, f32[128,1024]{1,0:T(8,128)S(1)}, u32[]{:S(2)}, u32[]{:S(2)}) %collective-permute-start.3) | collective-permute-done | bytes 524320 | tf_op jit(solution)/shard_map/ppermute | solution.py:79
  169.4 11.8 %collective-permute-done.4 = f32[128,1024]{1,0:T(8,128)S(1)} collective-permute-done((f32[128,1024]{1,0:T(8,128)S(1)}, f32[128,1024]{1,0:T(8,128)S(1)}, u32[]{:S(2)}, u32[]{:S(2)}) %collective-permute-start.4) | collective-permute-done | bytes 524320 | tf_op jit(solution)/shard_map/ppermute | solution.py:79
  181.3 2.5 collective-permute-start.5
  183.8 22.2 %collective-permute-done.5 = f32[128,1024]{1,0:T(8,128)S(1)} collective-permute-done((f32[128,1024]{1,0:T(8,128)S(1)}, f32[128,1024]{1,0:T(8,128)S(1)}, u32[]{:S(2)}, u32[]{:S(2)}) %collective-permute-start.5) | collective-permute-done | bytes 524320 | tf_op jit(solution)/shard_map/ppermute | solution.py:79
  206.3 5.3 %fusion.43 = f32[128,1024]{1,0:T(8,128)} fusion(f32[128,1024]{1,0:T(8,128)S(1)} %multiply_add_fusion.2, f32[1024,1024]{1,0:T(8,128)S(1)} %copy-done.1), kind=kOutput, calls=%fused_computation.66 | convolution fusion | flops 1610612736 | bytes 5242880 | tf_op jit(solution)/shard_map/ec,wc->ew/dot_general | solution.py:45
  211.9 22.0 %reduce-scatter.9.cloned.1.call-done = f32[32,1024]{1,0:T(8,128)} async-done(((f32[128,1024]{1,0:T(8,128)}), f32[32,1024]{1,0:T(8,128)}) %reduce-scatter.9.cloned.1.call-update) | async-done | bytes 131088 | tf_op jit(solution)/shard_map/reduce_scatter | solution.py:44
  234.9 6.8 %all_gather.18 = f32[128,1024]{1,0:T(8,128)S(1)} all-gather(f32[32,1024]{1,0:T(8,128)S(1)} %bitcast_add_fusion.1), channel_id=1, replica_groups=mesh['rows'=8,'cols'=4] {'cols'}, dimensions={0}, use_global_device_ids=true | all-gather | bytes 655360 | tf_op jit(solution)/shard_map/all_gather | solution.py:72
  241.8 4.7 %fusion.44 = f32[128,1024]{1,0:T(8,128)S(1)} fusion(f32[128,1024]{1,0:T(8,128)S(1)} %all_gather.18, f32[1024,1024]{1,0:T(8,128)} %param.7), kind=kOutput, calls=%fused_computation.67 | convolution fusion | flops 1610612736 | bytes 5242880 | tf_op jit(solution)/shard_map/dot_general | solution.py:71
  248.1 12.7 %collective-permute-done.6 = f32[128,1024]{1,0:T(8,128)S(1)} collective-permute-done((f32[128,1024]{1,0:T(8,128)S(1)}, f32[128,1024]{1,0:T(8,128)S(1)}, u32[]{:S(2)}, u32[]{:S(2)}) %collective-permute-start.6) | collective-permute-done | bytes 524320 | tf_op jit(solution)/shard_map/ppermute | solution.py:79
  262.4 11.8 %collective-permute-done.7 = f32[128,1024]{1,0:T(8,128)S(1)} collective-permute-done((f32[128,1024]{1,0:T(8,128)S(1)}, f32[128,1024]{1,0:T(8,128)S(1)}, u32[]{:S(2)}, u32[]{:S(2)}) %collective-permute-start.7) | collective-permute-done | bytes 524320 | tf_op jit(solution)/shard_map/ppermute | solution.py:79
  274.3 2.5 collective-permute-start.8
  276.8 22.2 %collective-permute-done.8 = f32[128,1024]{1,0:T(8,128)S(1)} collective-permute-done((f32[128,1024]{1,0:T(8,128)S(1)}, f32[128,1024]{1,0:T(8,128)S(1)}, u32[]{:S(2)}, u32[]{:S(2)}) %collective-permute-start.8) | collective-permute-done | bytes 524320 | tf_op jit(solution)/shard_map/ppermute | solution.py:79
  299.0 5.2 %fusion.38 = f32[128,1024]{1,0:T(8,128)} fusion(f32[1024,1024]{1,0:T(8,128)S(1)} %copy-done.2, f32[128,1024]{1,0:T(8,128)S(1)} %add.113, f32[128,1024]{1,0:T(8,128)S(1)} %collective-permute-done.8, f32[128,1024]{1,0:T(8,128)S(1)} %multiply_add_fusion.2, f32[1024]{0:T(1024)S(1)} %broadcast_subtract_fusion, f32[1024]{0:T(1024)S(1)} %copy-done.8), kind=kOutput, calls=%fused_computation.61 | convolution fusion | flops 1611137024 | bytes 6299648 | tf_op jit(solution)/shard_map/ec,wc->ew/dot_general | solution.py:45
  304.4 22.1 %reduce-scatter.11.cloned.1.call-done = f32[32,1024]{1,0:T(8,128)} async-done(((f32[128,1024]{1,0:T(8,128)}), f32[32,1024]{1,0:T(8,128)}) %reduce-scatter.11.cloned.1.call-update) | async-done | bytes 131088 | tf_op jit(solution)/shard_map/reduce_scatter | solution.py:44
  327.6 6.6 %all_gather.19 = f32[128,1024]{1,0:T(8,128)S(1)} all-gather(f32[32,1024]{1,0:T(8,128)S(1)} %bitcast_add_fusion), channel_id=1, replica_groups=mesh['rows'=8,'cols'=4] {'cols'}, dimensions={0}, use_global_device_ids=true | all-gather | bytes 655360 | tf_op jit(solution)/shard_map/all_gather | solution.py:72
  334.2 4.6 %fusion.45 = f32[128,1024]{1,0:T(8,128)S(1)} fusion(f32[128,1024]{1,0:T(8,128)S(1)} %all_gather.19, f32[1024,1024]{1,0:T(8,128)} %param.7), kind=kOutput, calls=%fused_computation.68 | convolution fusion | flops 1610612736 | bytes 5242880 | tf_op jit(solution)/shard_map/dot_general | solution.py:71
  340.4 12.7 %collective-permute-done.9 = f32[128,1024]{1,0:T(8,128)S(1)} collective-permute-done((f32[128,1024]{1,0:T(8,128)S(1)}, f32[128,1024]{1,0:T(8,128)S(1)}, u32[]{:S(2)}, u32[]{:S(2)}) %collective-permute-start.9) | collective-permute-done | bytes 524320 | tf_op jit(solution)/shard_map/ppermute | solution.py:79
  356.5 10.1 %collective-permute-done.10 = f32[128,1024]{1,0:T(8,128)S(1)} collective-permute-done((f32[128,1024]{1,0:T(8,128)S(1)}, f32[128,1024]{1,0:T(8,128)S(1)}, u32[]{:S(2)}, u32[]{:S(2)}) %collective-permute-start.10) | collective-permute-done | bytes 524320 | tf_op jit(solution)/shard_map/ppermute | solution.py:79
  366.6 2.5 collective-permute-start.11
  370.1 46.7 %all-reduce = f32[4,32,64]{1,0,2:T(4,128)S(1)} all-reduce(f32[4,32,64]{1,0,2:T(4,128)S(1)} %copy.30), channel_id=6, replica_groups=mesh['rows'=8,'cols'=4] {'rows'}, use_global_device_ids=true, to_apply=%region_9.10.clone | all-reduce | flops 8192 | bytes 65536
  (93 shorter events, 21.9 us)
Async XLA Ops:
  7.2 7.7 %copy-start.12 = (s32[8]{0:T(128)S(1)}, s32[8]{0:T(128)}, u32[]{:S(2)}) copy-start(s32[8]{0:T(128)} %param.11) | copy-start | bytes 100
  7.2 7.7 %copy-start.11 = (s32[64]{0:T(128)S(1)}, s32[64]{0:T(128)}, u32[]{:S(2)}) copy-start(s32[64]{0:T(128)} %param.12) | copy-start | bytes 772
  7.2 8.6 %copy-start.10 = (f32[4,128,8]{1,2,0:T(8,128)S(1)}, f32[4,128,8]{1,2,0:T(8,128)}, u32[]{:S(2)}) copy-start(f32[4,128,8]{1,2,0:T(8,128)} %param.13) | copy-start | bytes 49156
  7.2 41.3 %copy-start.9 = (f32[1024]{0:T(1024)S(1)}, f32[1024]{0:T(1024)}, u32[]{:S(2)}) copy-start(f32[1024]{0:T(1024)} %param.10) | copy-start | bytes 12292
  7.2 41.2 %reduce-scatter.5.cloned.1.call-start = ((), (), s32[]{:S(2)}) async-start(), calls=%async_computation.4 | async-start | bytes 655360 | tf_op jit(solution)/shard_map/reduce_scatter | solution.py:44
  14.8 126.3 %reduce-scatter.7.cloned.1.call-start = ((), (), s32[]{:S(2)}) async-start(), calls=%async_computation.5 | async-start | bytes 655360 | tf_op jit(solution)/shard_map/reduce_scatter | solution.py:44
  56.6 34.8 %copy-start.8 = (f32[1024]{0:T(1024)S(1)}, f32[1024]{0:T(1024)}, u32[]{:S(2)}) copy-start(f32[1024]{0:T(1024)} %param.9) | copy-start | bytes 12292
  56.6 57.3 %copy-start = (f32[1024,1024]{1,0:T(8,128)S(1)}, f32[1024,1024]{1,0:T(8,128)}, u32[]{:S(2)}) copy-start(f32[1024,1024]{1,0:T(8,128)} %param.7) | copy-start | bytes 12582916
  56.6 57.3 %copy-start.3 = (f32[128,1024]{1,0:T(8,128)S(1)}, f32[128,1024]{1,0:T(8,128)}, u32[]{:S(2)}) copy-start(f32[128,1024]{1,0:T(8,128)} %param.8) | copy-start | bytes 1572868
  61.4 14.2 %collective-permute-start = (f32[128,1024]{1,0:T(8,128)S(1)}, f32[128,1024]{1,0:T(8,128)S(1)}, u32[]{:S(2)}, u32[]{:S(2)}) collective-permute-start(f32[128,1024]{1,0:T(8,128)S(1)} %fusion.41), channel_id=1, source_target_pairs={{0,4},{4,0},{8,12},{12,8},{16,20},{20,16},{24,28},{28,24},{1,5},{5... | collective-permute-start | bytes 1572872 | tf_op jit(solution)/shard_map/ppermute | solution.py:79
  75.7 13.4 %collective-permute-start.1 = (f32[128,1024]{1,0:T(8,128)S(1)}, f32[128,1024]{1,0:T(8,128)S(1)}, u32[]{:S(2)}, u32[]{:S(2)}) collective-permute-start(f32[128,1024]{1,0:T(8,128)S(1)} %add.100), channel_id=1, source_target_pairs={{0,8},{4,12},{8,0},{12,4},{16,24},{20,28},{24,16},{28,20},{1,9},{5... | collective-permute-start | bytes 1572872 | tf_op jit(solution)/shard_map/ppermute | solution.py:79
  89.2 24.8 %collective-permute-start.2 = (f32[128,1024]{1,0:T(8,128)S(1)}, f32[128,1024]{1,0:T(8,128)S(1)}, u32[]{:S(2)}, u32[]{:S(2)}) collective-permute-start(f32[128,1024]{1,0:T(8,128)S(1)} %add.101), channel_id=1, source_target_pairs={{0,16},{4,20},{8,24},{12,28},{16,0},{20,4},{24,8},{28,12},{1,17},{... | collective-permute-start | bytes 1572872 | tf_op jit(solution)/shard_map/ppermute | solution.py:79
  119.1 114.8 %reduce-scatter.9.cloned.1.call-start = ((), (), s32[]{:S(2)}) async-start(), calls=%async_computation.6 | async-start | bytes 655360 | tf_op jit(solution)/shard_map/reduce_scatter | solution.py:44
  153.5 52.7 %copy-start.1 = (f32[1024,1024]{1,0:T(8,128)S(1)}, f32[1024,1024]{1,0:T(8,128)}, u32[]{:S(2)}) copy-start(f32[1024,1024]{1,0:T(8,128)} %param.7) | copy-start | bytes 12582916
  153.5 14.2 %collective-permute-start.3 = (f32[128,1024]{1,0:T(8,128)S(1)}, f32[128,1024]{1,0:T(8,128)S(1)}, u32[]{:S(2)}, u32[]{:S(2)}) collective-permute-start(f32[128,1024]{1,0:T(8,128)S(1)} %fusion.42), channel_id=1, source_target_pairs={{0,4},{4,0},{8,12},{12,8},{16,20},{20,16},{24,28},{28,24},{1,5},{5... | collective-permute-start | bytes 1572872 | tf_op jit(solution)/shard_map/ppermute | solution.py:79
  167.9 13.4 %collective-permute-start.4 = (f32[128,1024]{1,0:T(8,128)S(1)}, f32[128,1024]{1,0:T(8,128)S(1)}, u32[]{:S(2)}, u32[]{:S(2)}) collective-permute-start(f32[128,1024]{1,0:T(8,128)S(1)} %add.106), channel_id=1, source_target_pairs={{0,8},{4,12},{8,0},{12,4},{16,24},{20,28},{24,16},{28,20},{1,9},{5... | collective-permute-start | bytes 1572872 | tf_op jit(solution)/shard_map/ppermute | solution.py:79
  181.3 24.7 %collective-permute-start.5 = (f32[128,1024]{1,0:T(8,128)S(1)}, f32[128,1024]{1,0:T(8,128)S(1)}, u32[]{:S(2)}, u32[]{:S(2)}) collective-permute-start(f32[128,1024]{1,0:T(8,128)S(1)} %add.107), channel_id=1, source_target_pairs={{0,16},{4,20},{8,24},{12,28},{16,0},{20,4},{24,8},{28,12},{1,17},{... | collective-permute-start | bytes 1572872 | tf_op jit(solution)/shard_map/ppermute | solution.py:79
  211.5 115.0 %reduce-scatter.11.cloned.1.call-start = ((), (), s32[]{:S(2)}) async-start(), calls=%async_computation.7 | async-start | bytes 655360 | tf_op jit(solution)/shard_map/reduce_scatter | solution.py:44
  241.8 57.2 %copy-start.2 = (f32[1024,1024]{1,0:T(8,128)S(1)}, f32[1024,1024]{1,0:T(8,128)}, u32[]{:S(2)}) copy-start(f32[1024,1024]{1,0:T(8,128)} %param.7) | copy-start | bytes 12582916
  246.5 14.2 %collective-permute-start.6 = (f32[128,1024]{1,0:T(8,128)S(1)}, f32[128,1024]{1,0:T(8,128)S(1)}, u32[]{:S(2)}, u32[]{:S(2)}) collective-permute-start(f32[128,1024]{1,0:T(8,128)S(1)} %fusion.44), channel_id=1, source_target_pairs={{0,4},{4,0},{8,12},{12,8},{16,20},{20,16},{24,28},{28,24},{1,5},{5... | collective-permute-start | bytes 1572872 | tf_op jit(solution)/shard_map/ppermute | solution.py:79
  260.8 13.4 %collective-permute-start.7 = (f32[128,1024]{1,0:T(8,128)S(1)}, f32[128,1024]{1,0:T(8,128)S(1)}, u32[]{:S(2)}, u32[]{:S(2)}) collective-permute-start(f32[128,1024]{1,0:T(8,128)S(1)} %add.112), channel_id=1, source_target_pairs={{0,8},{4,12},{8,0},{12,4},{16,24},{20,28},{24,16},{28,20},{1,9},{5... | collective-permute-start | bytes 1572872 | tf_op jit(solution)/shard_map/ppermute | solution.py:79
  274.3 24.7 %collective-permute-start.8 = (f32[128,1024]{1,0:T(8,128)S(1)}, f32[128,1024]{1,0:T(8,128)S(1)}, u32[]{:S(2)}, u32[]{:S(2)}) collective-permute-start(f32[128,1024]{1,0:T(8,128)S(1)} %add.113), channel_id=1, source_target_pairs={{0,16},{4,20},{8,24},{12,28},{16,0},{20,4},{24,8},{28,12},{1,17},{... | collective-permute-start | bytes 1572872 | tf_op jit(solution)/shard_map/ppermute | solution.py:79
  304.1 50.6 %copy-start.13 = (u32[32]{0:T(128)S(1)}, u32[32]{0:T(128)}, u32[]{:S(2)}) copy-start(u32[32]{0:T(128)} %constant.42) | copy-start | bytes 388
  304.1 51.8 %copy-start.4 = (f32[32,1024]{1,0:T(8,128)S(1)}, f32[32,1024]{1,0:T(8,128)}, u32[]{:S(2)}) copy-start(f32[32,1024]{1,0:T(8,128)} %reduce-scatter.5.cloned.1.call-done) | copy-start | bytes 393220
  326.6 29.7 %copy-start.5 = (f32[32,1024]{1,0:T(8,128)S(1)}, f32[32,1024]{1,0:T(8,128)}, u32[]{:S(2)}) copy-start(f32[32,1024]{1,0:T(8,128)} %reduce-scatter.7.cloned.1.call-done) | copy-start | bytes 393220
  334.2 35.1 %copy-start.6 = (f32[32,1024]{1,0:T(8,128)S(1)}, f32[32,1024]{1,0:T(8,128)}, u32[]{:S(2)}) copy-start(f32[32,1024]{1,0:T(8,128)} %reduce-scatter.9.cloned.1.call-done) | copy-start | bytes 393220
  334.2 35.4 %copy-start.7 = (f32[32,1024]{1,0:T(8,128)S(1)}, f32[32,1024]{1,0:T(8,128)}, u32[]{:S(2)}) copy-start(f32[32,1024]{1,0:T(8,128)} %reduce-scatter.11.cloned.1.call-done) | copy-start | bytes 393220
  338.8 14.2 %collective-permute-start.9 = (f32[128,1024]{1,0:T(8,128)S(1)}, f32[128,1024]{1,0:T(8,128)S(1)}, u32[]{:S(2)}, u32[]{:S(2)}) collective-permute-start(f32[128,1024]{1,0:T(8,128)S(1)} %fusion.45), channel_id=1, source_target_pairs={{0,4},{4,0},{8,12},{12,8},{16,20},{20,16},{24,28},{28,24},{1,5},{5... | collective-permute-start | bytes 1572872 | tf_op jit(solution)/shard_map/ppermute | solution.py:79
  353.2 13.4 %collective-permute-start.10 = (f32[128,1024]{1,0:T(8,128)S(1)}, f32[128,1024]{1,0:T(8,128)S(1)}, u32[]{:S(2)}, u32[]{:S(2)}) collective-permute-start(f32[128,1024]{1,0:T(8,128)S(1)} %add.118), channel_id=1, source_target_pairs={{0,8},{4,12},{8,0},{12,4},{16,24},{20,28},{24,16},{28,20},{1,9},{5... | collective-permute-start | bytes 1572872 | tf_op jit(solution)/shard_map/ppermute | solution.py:79
  366.6 50.9 %collective-permute-start.11 = (f32[128,1024]{1,0:T(8,128)S(1)}, f32[128,1024]{1,0:T(8,128)S(1)}, u32[]{:S(2)}, u32[]{:S(2)}) collective-permute-start(f32[128,1024]{1,0:T(8,128)S(1)} %add.119), channel_id=1, source_target_pairs={{0,16},{4,20},{8,24},{12,28},{16,0},{20,4},{24,8},{28,12},{1,17},{... | collective-permute-start | bytes 1572872 | tf_op jit(solution)/shard_map/ppermute | solution.py:79
Sparse Core Ops, SparseCore 0:
  14.9 24.3 reduce-scatter.4
  119.2 21.8 reduce-scatter.6
  211.7 22.2 reduce-scatter.8
  304.3 22.2 reduce-scatter.10
